TPU v7x, 32 devices: a whole 2x2x4 slice. The times are simulated.
32 devices in a mesh: owner: 8 (over z, y), rows: 4 (over x, core).
Axes of the slice: x: 2, y: 2, z: 4, core: 2. Of those that a mesh axis runs over, the one named last changes fastest.
Arguments:
- master_down: float32 [16, 6400, 4096], P('owner', None, 'rows'), may hold values from -0.109375 to 0.109375
- router_weight: float32 [4096, 16], P('rows', 'owner'), may hold values from -0.09375 to 0.09375
- router_gain: float32 [4096], P('rows'), may hold values from 0.25 to 1.75
Outputs:
- final_down: bfloat16 [16, 6400, 4096], P('owner', 'rows')
- scale_down: float32 [16, 6400], P('owner', 'rows')
- serve_router: bfloat16 [4096, 16], replicated
All inputs are finite; a program needn't handle non-finite values. Where the computation divides by a largest or mean magnitude, that divisor is 1e-20 or more.
Results may differ from a plain program's by a relative error of at most 0.001.
Values may be sent and summed in bfloat16 or wider, within the bound.
No kernel may reach another device: no remote copies, remote signals or barrier semaphores. Data moves between devices by JAX's collectives and lax.ppermute only.
A program may use at most 192 MiB of HBM per device.

v0:
```python
import jax
import jax.numpy as jnp
from jax import lax
from jax.sharding import PartitionSpec as P

D_MODEL = 4096


def per_device(master_down, router_weight, router_gain):
    total_down = lax.psum(jnp.sum(jnp.abs(master_down), axis=2), "rows")
    scale_down = total_down / D_MODEL
    narrow_down = (master_down / jnp.expand_dims(scale_down, 2)).astype(jnp.bfloat16)
    final_down = lax.all_to_all(narrow_down, "rows", split_axis=1, concat_axis=2, tiled=True)
    scale_down = lax.dynamic_slice_in_dim(
        scale_down, lax.axis_index("rows") * final_down.shape[1], final_down.shape[1], axis=1
    )
    part_router = (router_weight * router_gain[:, None]).astype(jnp.bfloat16)
    row_router = lax.all_gather(part_router, "rows", axis=0, tiled=True)
    serve_router = lax.all_gather(row_router, "owner", axis=1, tiled=True)
    return (final_down, scale_down, serve_router)


def solution(mesh):
    return jax.shard_map(
        per_device,
        mesh=mesh,
        in_specs=(P("owner", None, "rows"), P("rows", "owner"), P("rows")),
        out_specs=(P("owner", "rows", None), P("owner", "rows"), P()),
        check_vma=False,
    )
```

profile of v0, /device:TPU:0, one launch (start us, length us, event | category | flops | bytes accessed | tf_op | source)
XLA Modules:
  0.0 506.3 jit_solution(15090514093543817720)
XLA Ops:
  0.6 17.0 %abs_reduce_fusion = f32[2,6400]{1,0:T(2,128)S(1)} fusion(f32[2,6400,1024]{2,1,0:T(8,128)} %param.3), kind=kLoop, calls=%fused_computation.1 | loop fusion | flops 26201600 | bytes 52480000 | tf_op jit(solution)/shard_map/reduce_sum | solution.py:10
  17.6 13.4 %psum.7 = f32[2,6400]{1,0:T(2,128)S(1)} all-reduce(f32[2,6400]{1,0:T(2,128)S(1)} %abs_reduce_fusion), channel_id=1, replica_groups=mesh['owner'=8,'rows'=4] {'rows'}, use_global_device_ids=true, to_apply=%region_1.0 | all-reduce | flops 12800 | bytes 102400 | tf_op jit(solution)/shard_map/psum | solution.py:10
  31.1 26.1 %divide_convert_fusion = bf16[2,6400,1024]{2,1,0:T(8,128)(2,1)} fusion(f32[2,6400,1024]{2,1,0:T(8,128)} %param.3, f32[2,6400]{1,0:T(2,128)S(1)} %broadcast_multiply_fusion), kind=kLoop, calls=%fused_computation | loop fusion | flops 26214400 | bytes 78694400 | tf_op jit(solution)/shard_map/convert_element_type | solution.py:12
  57.2 0.0 copy-start
  57.2 0.0 copy-start.1
  57.2 47.4 %copy.10 = bf16[2,6400,1024]{2,0,1:T(2,128)(2,1)} copy(bf16[2,6400,1024]{2,1,0:T(8,128)(2,1)} %divide_convert_fusion) | data formatting | bytes 52428800 | tf_op jit(solution)/shard_map/convert_element_type | solution.py:12
  104.6 8.6 %all-to-all-start = ((bf16[2,6400,1024]{2,0,1:T(2,128)(2,1)}), bf16[2,6400,1024]{2,0,1:T(2,128)(2,1)}, u32[]{:S(2)}, u32[]{:S(2)}) async-start(bf16[2,6400,1024]{2,0,1:T(2,128)(2,1)} %copy.10), calls=%async_computation | async-start | bytes 52428800 | tf_op jit(solution)/shard_map/all_to_all | solution.py:13
  113.2 0.0 copy-done
  113.2 0.0 copy-done.1
  113.2 285.0 %all_gather.6 = bf16[4096,2]{0,1:T(2,128)(2,1)S(1)} all-gather(bf16[1024,2]{0,1:T(2,128)(2,1)S(1)} %multiply_convert_fusion), channel_id=1, replica_groups=mesh['owner'=8,'rows'=4] {'rows'}, dimensions={0}, use_global_device_ids=true | all-gather | bytes 20480 | tf_op jit(solution)/shard_map/all_gather | solution.py:18
  398.2 30.9 %all-gather = bf16[8,2,4096]{2,1,0:T(2,128)(2,1)S(1)} all-gather(bf16[1,2,4096]{2,1,0:T(2,128)(2,1)S(1)} %bitcast.8), channel_id=1, replica_groups=mesh['owner'=8,'rows'=4] {'owner'}, dimensions={0}, use_global_device_ids=true | all-gather | bytes 147456 | tf_op jit(solution)/shard_map/all_gather | solution.py:19
  429.1 0.7 reshape.9
  429.8 0.7 constant_dynamic-slice_fusion
  430.5 0.0 all-to-all-done
  430.5 33.4 %copy.11 = bf16[2,1600,4,1024]{3,2,1,0:T(4,128)(2,1)} copy(bf16[2,1600,4,1024]{3,0,1,2:T(2,128)(2,1)} %bitcast.1) | data formatting | bytes 52428800 | tf_op jit(solution)/shard_map/all_to_all | solution.py:13
  463.9 42.5 %all_to_all.16 = bf16[2,1600,4096]{2,1,0:T(8,128)(2,1)} reshape(bf16[2,1600,4,1024]{3,2,1,0:T(4,128)(2,1)} %copy.11) | data formatting | bytes 52428800 | tf_op jit(solution)/shard_map/all_to_all | solution.py:13
  (2 shorter events, 0.0 us)
Async XLA Ops:
  57.2 56.0 %copy-start = (f32[1024,2]{0,1:T(2,128)S(1)}, f32[1024,2]{0,1:T(2,128)}, u32[]{:S(2)}) copy-start(f32[1024,2]{0,1:T(2,128)} %param.4) | copy-start | bytes 24580
  57.2 56.0 %copy-start.1 = (f32[1024]{0:T(1024)S(1)}, f32[1024]{0:T(1024)}, u32[]{:S(2)}) copy-start(f32[1024]{0:T(1024)} %param.5) | copy-start | bytes 12292
  104.6 325.9 %all-to-all-start = ((bf16[2,6400,1024]{2,0,1:T(2,128)(2,1)}), bf16[2,6400,1024]{2,0,1:T(2,128)(2,1)}, u32[]{:S(2)}, u32[]{:S(2)}) async-start(bf16[2,6400,1024]{2,0,1:T(2,128)(2,1)} %copy.10), calls=%async_computation | async-start | bytes 52428800 | tf_op jit(solution)/shard_map/all_to_all | solution.py:13
where the time goes:
time: 508 us; the launch traced here: 506 us
  blocking collectives  329 us (65%)
  local copies, waits for them, and re-layouts  125 us (25%)
  other arithmetic  43.2 us (9%)
  starting transfers between devices  8.59 us (2%)
    all_gather x1, blocking collectives, per_device(): row_router = lax.all_gather(part_router, 'rows', axis=0, tiled=True)  285 us
    all_to_all x2, local copies, waits for them, and re-layouts, per_device(): lax.all_to_all(narrow_down, 'rows', split_axis=1, concat_axis=2, tiled=True)  75.8 us
    convert_element_type x1, local copies, waits for them, and re-layouts, per_device(): (master_down / jnp.expand_dims(scale_down, 2)).astype(jnp.bfloat16)  47.4 us
    all_gather x1, blocking collectives, per_device(): serve_router = lax.all_gather(row_router, 'owner', axis=1, tiled=True)  30.9 us
    convert_element_type x1, other arithmetic, per_device(): (master_down / jnp.expand_dims(scale_down, 2)).astype(jnp.bfloat16)  26.1 us
    reduce_sum x1, other arithmetic, per_device(): total_down = lax.psum(jnp.sum(jnp.abs(master_down), axis=2), 'rows')  17 us
    psum x1, blocking collectives, per_device(): total_down = lax.psum(jnp.sum(jnp.abs(master_down), axis=2), 'rows')  13.4 us
  transfers between devices with their start and end apart: 1, of which 0 were waited for; matrix products, arithmetic and copies ran while one was open for 0% of the time, Pallas kernels for 0%

commit v1 on v0

v1 whole, which is shorter than its diff:
```python
import jax
import jax.numpy as jnp
from jax import lax
from jax.experimental import pallas as pl
from jax.experimental.pallas import tpu as pltpu
from jax.sharding import PartitionSpec as P


LANES, TILE = 128, 16
GROUPS = ((2, 2), (4, 4, 4), (5, 5, 5, 5, 5, 4, 3, 2))
AHEAD = 4
ROUTER_SENT, ROUTER_USED = 3, 7


def plan(rows):
    total, at, done, groups = sum(map(sum, GROUPS)), 0, 0, []
    for lengths in GROUPS:
        chunks = []
        for length in lengths:
            done += length
            end = rows if done == total else rows * done // total // TILE * TILE
            if end > at:
                chunks.append((at, end - at))
            at = end
        if chunks:
            groups.append(chunks)
    return groups


def block_of(first, count):
    return max((u for u in range(TILE, 81, TILE) if first % u == 0 and count % u == 0), default=count)


def tree_sum(terms):
    terms = list(terms)
    while len(terms) > 1:
        terms = [sum(terms[i + 1 : i + 2], terms[i]) for i in range(0, len(terms), 2)]
    return terms[0]


def narrow(out, blocks, sums, base, places, first, count, after):
    experts, n, rows, width = blocks.shape
    model = n * width
    step = block_of(first, count)

    def body(places_ref, *refs):
        ins, sums_refs = refs[:n], refs[n : 2 * n]
        outs, factors = refs[-n - 1 : -1], refs[-1]
        e, i = pl.program_id(0), pl.program_id(1)

        @pl.when(i == 0)
        def _():
            inverse = 1.0 / (tree_sum(r[e, :, first - base : first - base + count] for r in sums_refs) / model)
            row = lax.broadcasted_iota(jnp.int32, inverse.shape, 0)
            for k in range(n):
                chosen = jnp.sum(jnp.where(row == places_ref[k], inverse, 0.0), axis=0, keepdims=True)
                factors[k] = jnp.broadcast_to(chosen, (LANES, count)).T

        rows_now = pl.ds(pl.multiple_of(i * step, step), step)
        for k in range(n):
            factor = factors[k, rows_now, :]
            for j in range(0, width, LANES):
                outs[k][0, :, j : j + LANES] = (ins[k][0, 0, :, j : j + LANES] * factor).astype(jnp.bfloat16)

    def reader(k):
        return pl.BlockSpec((1, 1, step, width), lambda e, i, p: (e, p[k], first // step + i, 0))

    whole = pl.BlockSpec(sums[0].shape, lambda e, i, p: (0, 0, 0))
    in_specs = [reader(k) for k in range(n)] + [whole] * n
    args = [blocks] * n + list(sums)
    aliases = {}
    if out is not None:
        aliases = {len(args) + 1: 0}
        args.append(out)
        in_specs.append(pl.BlockSpec(memory_space=pltpu.HBM))
    args += after
    in_specs += [pl.BlockSpec(memory_space=pl.ANY)] * len(after)
    peer_shape = jax.ShapeDtypeStruct((experts, count, width), jnp.bfloat16)
    peer_spec = pl.BlockSpec((1, step, width), lambda e, i, p: (e, i, 0))
    own_spec = pl.BlockSpec((1, step, width), lambda e, i, p: (e, first // step + i, p[n]))
    bytes_moved = 6 * n * experts * count * width
    return pl.pallas_call(
        body,
        out_shape=[jax.ShapeDtypeStruct((experts, rows, n * width), jnp.bfloat16)] + [peer_shape] * (n - 1),
        grid_spec=pltpu.PrefetchScalarGridSpec(
            num_scalar_prefetch=1,
            grid=(experts, count // step),
            in_specs=in_specs,
            out_specs=[own_spec] + [peer_spec] * (n - 1),
            scratch_shapes=[pltpu.VMEM((n, count, LANES), jnp.float32)],
        ),
        input_output_aliases=aliases,
        cost_estimate=pl.CostEstimate(flops=bytes_moved, bytes_accessed=bytes_moved, transcendentals=0),
    )(places, *args)


def place(out, pieces, sources, first):
    experts, count, width = pieces[0].shape
    m = len(pieces)

    def body(sources_ref, *refs):
        ins, o = refs[:m], refs[m + 1]
        held, in_sems, out_sems = refs[m + 2 :]
        every = [(k, e) for k in range(m) for e in range(experts)]
        loads = [pltpu.make_async_copy(ins[k].at[e], held.at[k, e], in_sems.at[k, e]) for k, e in every]
        stores = []
        for k, e in every:
            column = pl.multiple_of(sources_ref[k + 1] * width, width)
            target = o.at[e, pl.ds(first, count), pl.ds(column, width)]
            stores.append(pltpu.make_async_copy(held.at[k, e], target, out_sems.at[k, e]))
        for load in loads:
            load.start()
        for load, store in zip(loads, stores):
            load.wait()
            store.start()
        for store in stores:
            store.wait()

    anywhere = pl.BlockSpec(memory_space=pltpu.HBM)
    bytes_moved = 4 * m * experts * count * width
    return pl.pallas_call(
        body,
        out_shape=jax.ShapeDtypeStruct(out.shape, out.dtype),
        grid_spec=pltpu.PrefetchScalarGridSpec(
            num_scalar_prefetch=1,
            grid=(),
            in_specs=[anywhere] * (m + 1),
            out_specs=anywhere,
            scratch_shapes=[
                pltpu.VMEM((m, experts, count, width), jnp.bfloat16),
                pltpu.SemaphoreType.DMA((m, experts)),
                pltpu.SemaphoreType.DMA((m, experts)),
            ],
        ),
        input_output_aliases={m + 1: 0},
        cost_estimate=pl.CostEstimate(flops=bytes_moved, bytes_accessed=bytes_moved, transcendentals=0),
    )(sources, *pieces, out)


def per_device(master_down, router_weight, router_gain):
    n = lax.axis_size("rows")
    me = lax.axis_index("rows")
    experts, total_rows, width = master_down.shape
    rows = total_rows // n
    model = width * n
    groups = plan(rows)
    blocks = master_down.reshape(experts, n, rows, width)
    if n & (n - 1):
        hops = [[(i, (i + k) % n) for i in range(n)] for k in range(n)]
        targets = [(me + k) % n for k in range(n)]
        sources = [(me + n - k) % n for k in range(n)]
    else:
        hops = [[(i, i ^ k) for i in range(n)] for k in range(n)]
        targets = sources = [me ^ k for k in range(n)]
    target_list = jnp.stack(targets + [me]).astype(jnp.int32)
    source_list = target_list if sources is targets else jnp.stack(sources + [me]).astype(jnp.int32)
    far_first = list(range(n - 1, 0, -1))

    def exchange(x):
        got = {k: lax.ppermute(x, "rows", hops[k]) for k in far_first}
        return [x] + [got[k] for k in range(1, n)]

    def local_sums(source, group):
        return jnp.sum(jnp.abs(source[:, :, group[0][0] : sum(group[-1])]), axis=3)

    def shared_sums(g, source):
        sums = local_sums(source, groups[g])
        return exchange(sums)

    out, flying, after, router_rows = None, [], [], None
    serve_router = scale_down = None
    shared = [shared_sums(0, blocks)]
    c, chunks = 0, sum(map(len, groups))
    for g, group in enumerate(groups):
        for i, (first, count) in enumerate(group):
            if c == min(ROUTER_USED, chunks - 1):
                router_rows = lax.optimization_barrier((router_rows, sent[0]))[0]
                ordered = jnp.zeros((n,) + router_rows[0].shape, router_rows[0].dtype)
                for place_of, rows_of in zip(sources, router_rows):
                    ordered = lax.dynamic_update_index_in_dim(ordered, rows_of, place_of, 0)
                row_router = ordered.reshape(n * router_weight.shape[0], router_weight.shape[1])
                serve_router = lax.all_gather(row_router, "owner", axis=1, tiled=True)
                own = [tree_sum(lax.dynamic_index_in_dim(s, me, 1, keepdims=False) for s in sums) for sums in shared]
                scale_down = jnp.concatenate(own, axis=1) / model
                after = [serve_router, scale_down]
            out, *sent = narrow(out, blocks, shared[g], group[0][0], target_list, first, count, after)
            after = []
            if i == min(1, len(group) - 1) and g + 1 < len(groups):
                late = lax.optimization_barrier((blocks, sent[0]))[0]
                shared.append(shared_sums(g + 1, late))
            if c == min(ROUTER_SENT, chunks - 2):
                weight, gain, _ = lax.optimization_barrier((router_weight, router_gain, sent[0]))
                router_rows = exchange((weight * gain[:, None]).astype(jnp.bfloat16))
            got = {k: lax.ppermute(sent[k - 1], "rows", hops[k]) for k in far_first}
            flying.append(([got[k] for k in range(1, n)], first))
            if len(flying) > AHEAD:
                out = place(out, flying[0][0], source_list, flying.pop(0)[1])
            c += 1
    for pieces, first in flying:
        out = place(out, pieces, source_list, first)
    return out, scale_down, serve_router


def solution(mesh):
    return jax.shard_map(
        per_device,
        mesh=mesh,
        in_specs=(P("owner", None, "rows"), P("rows", "owner"), P("rows")),
        out_specs=(P("owner", "rows", None), P("owner", "rows"), P()),
        check_vma=False,
    )
```

time: 508 us -> 345 us (0.68)
  blocking collectives: 329 us -> 31 us
  waiting for transfers between devices: 0.01 us -> 123 us
  Pallas kernels: 0 us -> 117 us
  local copies, waits for them, and re-layouts: 125 us -> 9.55 us
  starting transfers between devices: 8.59 us -> 36.1 us
  other arithmetic: 43.2 us -> 23.8 us
    all_gather x1 -> x0, blocking collectives: 285 us -> none  [per_device(): row_router = lax.all_gather(part_router, 'rows', axis=0, tiled=True)]
    ppermute x0 -> x51, waiting for transfers between devices: none -> 123 us  [the longest x39 112 us: per_device(): got = {k: lax.ppermute(sent[k - 1], 'rows', hops[k]) for k in far_first}]
    pallas_call x0 -> x26, Pallas kernels: none -> 117 us  [the longest x13 80.2 us: narrow(): pl.pallas_call(body, out_shape=[jax.ShapeDtypeStruct((experts, rows, n *...]
    all_to_all x2 -> x0, local copies, waits for them, and re-layouts: 75.8 us -> none  [per_device(): lax.all_to_all(narrow_down, 'rows', split_axis=1, concat_axis=2, tiled=True)]
    convert_element_type x1 -> x0, local copies, waits for them, and re-layouts: 47.4 us -> none  [per_device(): (master_down / jnp.expand_dims(scale_down, 2)).astype(jnp.bfloat16)]
    ppermute x0 -> x51, starting transfers between devices: none -> 36.1 us  [the longest x39 27.4 us: per_device(): got = {k: lax.ppermute(sent[k - 1], 'rows', hops[k]) for k in far_first}]
    convert_element_type x2 -> x1, other arithmetic: 26.1 us -> 0.01 us  [per_device(): router_rows = exchange((weight * gain[:, None]).astype(jnp.bfloat16))]
    psum x1 -> x0, blocking collectives: 13.4 us -> none  [per_device(): total_down = lax.psum(jnp.sum(jnp.abs(master_down), axis=2), 'rows')]
  transfers between devices with their start and end apart: 1 -> 51, of which waited for: 0 -> 19; matrix products, arithmetic and copies ran while one was open for 0% -> 6% of each run, Pallas kernels for 0% -> 32%
where the time goes in v1:
time: 345 us; the launch traced here: 342 us
  waiting for transfers between devices  123 us (36%)
  Pallas kernels  117 us (34%)
  starting transfers between devices  36.1 us (10%)
  blocking collectives  31 us (9%)
  other arithmetic  23.8 us (7%)
  local copies, waits for them, and re-layouts  9.55 us (3%)
    ppermute x39, waiting for transfers between devices, per_device(): got = {k: lax.ppermute(sent[k - 1], 'rows', hops[k]) for k in far_first}  112 us
    pallas_call x13, Pallas kernels, narrow(): pl.pallas_call(body, out_shape=[jax.ShapeDtypeStruct((experts, rows, n *...  80.2 us
    pallas_call x13, Pallas kernels, place(): pl.pallas_call(body, out_shape=jax.ShapeDtypeStruct(out.shape, out.dtype)...  37.1 us
    all_gather x1, blocking collectives, per_device(): serve_router = lax.all_gather(row_router, 'owner', axis=1, tiled=True)  31 us
    ppermute x39, starting transfers between devices, per_device(): got = {k: lax.ppermute(sent[k - 1], 'rows', hops[k]) for k in far_first}  27.4 us
    reduce_sum x3, other arithmetic, local_sums(): return jnp.sum(jnp.abs(source[:, :, group[0][0]:sum(group[-1])]), axis=3)  21 us
    ppermute x12, waiting for transfers between devices, exchange(): got = {k: lax.ppermute(x, 'rows', hops[k]) for k in far_first}  10.8 us
    ppermute x12, starting transfers between devices, exchange(): got = {k: lax.ppermute(x, 'rows', hops[k]) for k in far_first}  8.71 us
  transfers between devices with their start and end apart: 51, of which 19 were waited for; matrix products, arithmetic and copies ran while one was open for 6% of the time, Pallas kernels for 32%

profile of v1, /device:TPU:0, one launch (start us, length us, event | category | flops | bytes accessed | tf_op | source)
XLA Modules:
  0.0 342.2 jit_solution(407974397781387636)
XLA Ops:
  17.2 5.6 %abs_reduce_fusion.1.refs_4_ = f32[2,4,384]{2,1,0:T(4,128)S(1)} fusion(f32[2,4,1600,1024]{3,2,1,0:T(8,128)} %bitcast.35), kind=kLoop, calls=%fused_computation.1 | loop fusion | flops 6288384 | bytes 12595200 | tf_op jit(solution)/shard_map/reduce_sum | solution.py:164
  28.5 5.0 %shard_map.60 = (bf16[2,1600,4096]{2,1,0:T(8,128)(2,1)}, bf16[2,128,1024]{2,1,0:T(8,128)(2,1)}, bf16[2,128,1024]{2,1,0:T(8,128)(2,1)}, bf16[2,128,1024]{2,1,0:T(8,128)(2,1)}) custom-call(s32[5]{0:T(128)} %stack.20.places_ref.sources_ref, f32[2,4,1600,1024]{3,2,1,0:T(8,128)} %bitcast.36, ...), custom_call_target="tpu_custom_call", output_to_operand_aliasing={{0}: (9, {})} | custom-call | flops 6291456 | bytes 6291456 | tf_op jit(solution)/shard_map/pallas_call | solution.py:82
  33.5 5.0 %shard_map.61 = (bf16[2,1600,4096]{2,1,0:T(8,128)(2,1)}, bf16[2,128,1024]{2,1,0:T(8,128)(2,1)}, bf16[2,128,1024]{2,1,0:T(8,128)(2,1)}, bf16[2,128,1024]{2,1,0:T(8,128)(2,1)}) custom-call(s32[5]{0:T(128)} %stack.20.places_ref.sources_ref, f32[2,4,1600,1024]{3,2,1,0:T(8,128)} %bitcast.40, ...), custom_call_target="tpu_custom_call", output_to_operand_aliasing={{0}: (9, {})} | custom-call | flops 6291456 | bytes 6291456 | tf_op jit(solution)/shard_map/pallas_call | solution.py:82
  38.5 12.9 %abs_reduce_fusion.refs_4_ = f32[2,4,1088]{2,1,0:T(4,128)S(1)} fusion(f32[2,4,1600,1024]{3,2,1,0:T(8,128)} %bitcast.44), kind=kLoop, calls=%fused_computation | loop fusion | flops 17817088 | bytes 35686400 | tf_op jit(solution)/shard_map/reduce_sum | solution.py:164
  68.6 5.2 %collective-permute-done.13.refs_1_ = bf16[2,64,1024]{2,1,0:T(8,128)(2,1)S(1)} collective-permute-done((bf16[2,64,1024]{2,1,0:T(8,128)(2,1)S(1)}, bf16[2,64,1024]{2,1,0:T(8,128)(2,1)S(1)}, u32[]{:S(2)}, u32[]{:S(2)}) %collective-permute-start.13) | collective-permute-done | bytes 262176 | tf_op jit(solution)/shard_map/ppermute | solution.py:194
  73.8 24.5 %collective-permute-done.14.refs_2_ = bf16[2,64,1024]{2,1,0:T(8,128)(2,1)S(1)} collective-permute-done((bf16[2,64,1024]{2,1,0:T(8,128)(2,1)S(1)}, bf16[2,64,1024]{2,1,0:T(8,128)(2,1)S(1)}, u32[]{:S(2)}, u32[]{:S(2)}) %collective-permute-start.14) | collective-permute-done | bytes 262176 | tf_op jit(solution)/shard_map/ppermute | solution.py:194
  101.8 5.0 %shard_map.62 = (bf16[2,1600,4096]{2,1,0:T(8,128)(2,1)}, bf16[2,128,1024]{2,1,0:T(8,128)(2,1)}, bf16[2,128,1024]{2,1,0:T(8,128)(2,1)}, bf16[2,128,1024]{2,1,0:T(8,128)(2,1)}) custom-call(s32[5]{0:T(128)} %stack.20.places_ref.sources_ref, f32[2,4,1600,1024]{3,2,1,0:T(8,128)} %bitcast.45, ...), custom_call_target="tpu_custom_call", output_to_operand_aliasing={{0}: (9, {})} | custom-call | flops 6291456 | bytes 6291456 | tf_op jit(solution)/shard_map/pallas_call | solution.py:82
  108.4 5.2 %collective-permute-done.34.refs_1_ = bf16[2,128,1024]{2,1,0:T(8,128)(2,1)S(1)} collective-permute-done((bf16[2,128,1024]{2,1,0:T(8,128)(2,1)}, bf16[2,128,1024]{2,1,0:T(8,128)(2,1)S(1)}, u32[]{:S(2)}, u32[]{:S(2)}) %collective-permute-start.34) | collective-permute-done | bytes 524320 | tf_op jit(solution)/shard_map/ppermute | solution.py:194
  117.5 8.5 %shard_map.64 = (bf16[2,1600,4096]{2,1,0:T(8,128)(2,1)}, bf16[2,160,1024]{2,1,0:T(8,128)(2,1)}, bf16[2,160,1024]{2,1,0:T(8,128)(2,1)}, bf16[2,160,1024]{2,1,0:T(8,128)(2,1)}) custom-call(s32[5]{0:T(128)} %stack.20.places_ref.sources_ref, f32[2,4,1600,1024]{3,2,1,0:T(8,128)} %bitcast.49, ...), custom_call_target="tpu_custom_call", output_to_operand_aliasing={{0}: (9, {})} | custom-call | flops 7864320 | bytes 7864320 | tf_op jit(solution)/shard_map/pallas_call | solution.py:82
  128.6 8.8 %shard_map.66 = (bf16[2,1600,4096]{2,1,0:T(8,128)(2,1)}, bf16[2,160,1024]{2,1,0:T(8,128)(2,1)}, bf16[2,160,1024]{2,1,0:T(8,128)(2,1)}, bf16[2,160,1024]{2,1,0:T(8,128)(2,1)}) custom-call(s32[5]{0:T(128)} %stack.20.places_ref.sources_ref, f32[2,4,1600,1024]{3,2,1,0:T(8,128)} %bitcast.53, ...), custom_call_target="tpu_custom_call", output_to_operand_aliasing={{0}: (9, {})} | custom-call | flops 7864320 | bytes 7864320 | tf_op jit(solution)/shard_map/pallas_call | solution.py:82
  142.7 5.6 %collective-permute-done.32.refs_2_ = bf16[2,128,1024]{2,1,0:T(8,128)(2,1)} collective-permute-done((bf16[2,128,1024]{2,1,0:T(8,128)(2,1)}, bf16[2,128,1024]{2,1,0:T(8,128)(2,1)}, u32[]{:S(2)}, u32[]{:S(2)}) %collective-permute-start.32) | collective-permute-done | bytes 524320 | tf_op jit(solution)/shard_map/ppermute | solution.py:194
  150.2 31.0 %all-gather = bf16[8,2,4096]{2,1,0:T(2,128)(2,1)S(1)} all-gather(bf16[1,2,4096]{2,1,0:T(2,128)(2,1)S(1)} %bitcast.83), channel_id=1, replica_groups=mesh['owner'=8,'rows'=4] {'owner'}, dimensions={0}, use_global_device_ids=true | all-gather | bytes 147456 | tf_op jit(solution)/shard_map/all_gather | solution.py:182
  185.5 8.6 %shard_map.68 = (bf16[2,1600,4096]{2,1,0:T(8,128)(2,1)}, bf16[2,160,1024]{2,1,0:T(8,128)(2,1)}, bf16[2,160,1024]{2,1,0:T(8,128)(2,1)}, bf16[2,160,1024]{2,1,0:T(8,128)(2,1)}) custom-call(s32[5]{0:T(128)} %stack.20.places_ref.sources_ref, f32[2,4,1600,1024]{3,2,1,0:T(8,128)} %bitcast.57, ...), custom_call_target="tpu_custom_call", output_to_operand_aliasing={{0}: (9, {})} | custom-call | flops 7864320 | bytes 7864320 | tf_op jit(solution)/shard_map/pallas_call | solution.py:82
  199.1 8.6 %shard_map.70 = (bf16[2,1600,4096]{2,1,0:T(8,128)(2,1)}, bf16[2,160,1024]{2,1,0:T(8,128)(2,1)}, bf16[2,160,1024]{2,1,0:T(8,128)(2,1)}, bf16[2,160,1024]{2,1,0:T(8,128)(2,1)}) custom-call(s32[5]{0:T(128)} %stack.20.places_ref.sources_ref, f32[2,4,1600,1024]{3,2,1,0:T(8,128)} %bitcast.61, ...), custom_call_target="tpu_custom_call", output_to_operand_aliasing={{0}: (9, {})} | custom-call | flops 7864320 | bytes 7864320 | tf_op jit(solution)/shard_map/pallas_call | solution.py:82
  211.3 8.5 %shard_map.72 = (bf16[2,1600,4096]{2,1,0:T(8,128)(2,1)}, bf16[2,160,1024]{2,1,0:T(8,128)(2,1)}, bf16[2,160,1024]{2,1,0:T(8,128)(2,1)}, bf16[2,160,1024]{2,1,0:T(8,128)(2,1)}) custom-call(s32[5]{0:T(128)} %stack.20.places_ref.sources_ref, f32[2,4,1600,1024]{3,2,1,0:T(8,128)} %bitcast.65, ...), custom_call_target="tpu_custom_call", output_to_operand_aliasing={{0}: (9, {})} | custom-call | flops 7864320 | bytes 7864320 | tf_op jit(solution)/shard_map/pallas_call | solution.py:82
  222.0 10.5 %collective-permute-done.23.refs_2_ = bf16[2,160,1024]{2,1,0:T(8,128)(2,1)} collective-permute-done((bf16[2,160,1024]{2,1,0:T(8,128)(2,1)}, bf16[2,160,1024]{2,1,0:T(8,128)(2,1)}, u32[]{:S(2)}, u32[]{:S(2)}) %collective-permute-start.23) | collective-permute-done | bytes 655392 | tf_op jit(solution)/shard_map/ppermute | solution.py:194
  236.5 7.3 %shard_map.74 = (bf16[2,1600,4096]{2,1,0:T(8,128)(2,1)}, bf16[2,128,1024]{2,1,0:T(8,128)(2,1)}, bf16[2,128,1024]{2,1,0:T(8,128)(2,1)}, bf16[2,128,1024]{2,1,0:T(8,128)(2,1)}) custom-call(s32[5]{0:T(128)} %stack.20.places_ref.sources_ref, f32[2,4,1600,1024]{3,2,1,0:T(8,128)} %bitcast.69, ...), custom_call_target="tpu_custom_call", output_to_operand_aliasing={{0}: (9, {})} | custom-call | flops 6291456 | bytes 6291456 | tf_op jit(solution)/shard_map/pallas_call | solution.py:82
  246.8 5.1 %shard_map.76 = (bf16[2,1600,4096]{2,1,0:T(8,128)(2,1)}, bf16[2,96,1024]{2,1,0:T(8,128)(2,1)}, bf16[2,96,1024]{2,1,0:T(8,128)(2,1)}, bf16[2,96,1024]{2,1,0:T(8,128)(2,1)}) custom-call(s32[5]{0:T(128)} %stack.20.places_ref.sources_ref, f32[2,4,1600,1024]{3,2,1,0:T(8,128)} %bitcast.73, f32[2,4,1600,1024]{3,2,1,0:T(8,128)} %bitcast.74, ...), custom_call_target="tpu_custom_call", output_to_operand_aliasing={{0}: (9, {})} | custom-call | flops 4718592 | bytes 4718592 | tf_op jit(solution)/shard_map/pallas_call | solution.py:82
  253.2 7.4 %collective-permute-done.50.refs_2_ = bf16[2,160,1024]{2,1,0:T(8,128)(2,1)} collective-permute-done((bf16[2,160,1024]{2,1,0:T(8,128)(2,1)}, bf16[2,160,1024]{2,1,0:T(8,128)(2,1)}, u32[]{:S(2)}, u32[]{:S(2)}) %collective-permute-start.50) | collective-permute-done | bytes 655392 | tf_op jit(solution)/shard_map/ppermute | solution.py:194
  261.5 12.3 %collective-permute-done.46.refs_1_ = bf16[2,160,1024]{2,1,0:T(8,128)(2,1)} collective-permute-done((bf16[2,160,1024]{2,1,0:T(8,128)(2,1)}, bf16[2,160,1024]{2,1,0:T(8,128)(2,1)}, u32[]{:S(2)}, u32[]{:S(2)}) %collective-permute-start.46) | collective-permute-done | bytes 655392 | tf_op jit(solution)/shard_map/ppermute | solution.py:194
  275.0 13.7 %collective-permute-done.47.refs_2_ = bf16[2,160,1024]{2,1,0:T(8,128)(2,1)} collective-permute-done((bf16[2,160,1024]{2,1,0:T(8,128)(2,1)}, bf16[2,160,1024]{2,1,0:T(8,128)(2,1)}, u32[]{:S(2)}, u32[]{:S(2)}) %collective-permute-start.47) | collective-permute-done | bytes 655392 | tf_op jit(solution)/shard_map/ppermute | solution.py:194
  300.4 10.7 %collective-permute-done.44.refs_2_ = bf16[2,128,1024]{2,1,0:T(8,128)(2,1)S(1)} collective-permute-done((bf16[2,128,1024]{2,1,0:T(8,128)(2,1)S(1)}, bf16[2,128,1024]{2,1,0:T(8,128)(2,1)S(1)}, u32[]{:S(2)}, u32[]{:S(2)}) %collective-permute-start.44) | collective-permute-done | bytes 524320 | tf_op jit(solution)/shard_map/ppermute | solution.py:194
  320.3 7.7 %collective-permute-done.41.refs_2_ = bf16[2,96,1024]{2,1,0:T(8,128)(2,1)S(1)} collective-permute-done((bf16[2,96,1024]{2,1,0:T(8,128)(2,1)}, bf16[2,96,1024]{2,1,0:T(8,128)(2,1)S(1)}, u32[]{:S(2)}, u32[]{:S(2)}) %collective-permute-start.41) | collective-permute-done | bytes 393248 | tf_op jit(solution)/shard_map/ppermute | solution.py:194
  332.7 6.1 %collective-permute-done.38.refs_2_ = bf16[2,64,1024]{2,1,0:T(8,128)(2,1)S(1)} collective-permute-done((bf16[2,64,1024]{2,1,0:T(8,128)(2,1)}, bf16[2,64,1024]{2,1,0:T(8,128)(2,1)S(1)}, u32[]{:S(2)}, u32[]{:S(2)}) %collective-permute-start.38) | collective-permute-done | bytes 262176 | tf_op jit(solution)/shard_map/ppermute | solution.py:194
  (243 shorter events, 111.7 us)
Async XLA Ops:
  24.7 40.8 %collective-permute-start.15 = (bf16[2,64,1024]{2,1,0:T(8,128)(2,1)S(1)}, bf16[2,64,1024]{2,1,0:T(8,128)(2,1)S(1)}, u32[]{:S(2)}, u32[]{:S(2)}) collective-permute-start(bf16[2,64,1024]{2,1,0:T(8,128)(2,1)S(1)} %copy-done.53), channel_id=1, source_target_pairs={{0,1},{1,0},{2,3},{3,2},{4,5},{5,4},{6,7},{7,6},{8,9},{9,8},{10,11... | collective-permute-start | bytes 786440 | tf_op jit(solution)/shard_map/ppermute | solution.py:194
  24.7 42.1 %collective-permute-start.16 = (bf16[2,64,1024]{2,1,0:T(8,128)(2,1)S(1)}, bf16[2,64,1024]{2,1,0:T(8,128)(2,1)S(1)}, u32[]{:S(2)}, u32[]{:S(2)}) collective-permute-start(bf16[2,64,1024]{2,1,0:T(8,128)(2,1)S(1)} %copy-done.52), channel_id=1, source_target_pairs={{0,2},{1,3},{2,0},{3,1},{4,6},{5,7},{6,4},{7,5},{8,10},{9,11},{10,... | collective-permute-start | bytes 786440 | tf_op jit(solution)/shard_map/ppermute | solution.py:194
  25.9 41.5 %collective-permute-start.17 = (bf16[2,64,1024]{2,1,0:T(8,128)(2,1)S(1)}, bf16[2,64,1024]{2,1,0:T(8,128)(2,1)S(1)}, u32[]{:S(2)}, u32[]{:S(2)}) collective-permute-start(bf16[2,64,1024]{2,1,0:T(8,128)(2,1)S(1)} %copy-done.51), channel_id=1, source_target_pairs={{0,3},{1,2},{2,1},{3,0},{4,7},{5,6},{6,5},{7,4},{8,11},{9,10},{10,... | collective-permute-start | bytes 786440 | tf_op jit(solution)/shard_map/ppermute | solution.py:194
  65.5 41.4 %collective-permute-start.9 = (bf16[2,128,1024]{2,1,0:T(8,128)(2,1)}, bf16[2,128,1024]{2,1,0:T(8,128)(2,1)S(1)}, u32[]{:S(2)}, u32[]{:S(2)}) collective-permute-start(bf16[2,128,1024]{2,1,0:T(8,128)(2,1)} %get-tuple-element.70), channel_id=1, source_target_pairs={{0,1},{1,0},{2,3},{3,2},{4,5},{5,4},{6,7},{7,6},{8,9},{9,8},{10,11... | collective-permute-start | bytes 1572872 | tf_op jit(solution)/shard_map/ppermute | solution.py:194
  65.5 41.5 %collective-permute-start.10 = (bf16[2,128,1024]{2,1,0:T(8,128)(2,1)}, bf16[2,128,1024]{2,1,0:T(8,128)(2,1)S(1)}, u32[]{:S(2)}, u32[]{:S(2)}) collective-permute-start(bf16[2,128,1024]{2,1,0:T(8,128)(2,1)} %get-tuple-element.71), channel_id=1, source_target_pairs={{0,2},{1,3},{2,0},{3,1},{4,6},{5,7},{6,4},{7,5},{8,10},{9,11},{10,... | collective-permute-start | bytes 1572872 | tf_op jit(solution)/shard_map/ppermute | solution.py:194
  66.8 40.8 %collective-permute-start.11 = (bf16[2,128,1024]{2,1,0:T(8,128)(2,1)}, bf16[2,128,1024]{2,1,0:T(8,128)(2,1)S(1)}, u32[]{:S(2)}, u32[]{:S(2)}) collective-permute-start(bf16[2,128,1024]{2,1,0:T(8,128)(2,1)} %get-tuple-element.72), channel_id=1, source_target_pairs={{0,3},{1,2},{2,1},{3,0},{4,7},{5,6},{6,5},{7,4},{8,11},{9,10},{10,... | collective-permute-start | bytes 1572872 | tf_op jit(solution)/shard_map/ppermute | solution.py:194
  100.2 37.2 %collective-permute-start.35 = (bf16[2,128,1024]{2,1,0:T(8,128)(2,1)}, bf16[2,128,1024]{2,1,0:T(8,128)(2,1)}, u32[]{:S(2)}, u32[]{:S(2)}) collective-permute-start(bf16[2,128,1024]{2,1,0:T(8,128)(2,1)} %get-tuple-element.101), channel_id=1, source_target_pairs={{0,3},{1,2},{2,1},{3,0},{4,7},{5,6},{6,5},{7,4},{8,11},{9,10},{10,... | collective-permute-start | bytes 1572872 | tf_op jit(solution)/shard_map/ppermute | solution.py:194
  113.6 34.7 %collective-permute-start.32 = (bf16[2,128,1024]{2,1,0:T(8,128)(2,1)}, bf16[2,128,1024]{2,1,0:T(8,128)(2,1)}, u32[]{:S(2)}, u32[]{:S(2)}) collective-permute-start(bf16[2,128,1024]{2,1,0:T(8,128)(2,1)} %get-tuple-element.99), channel_id=1, source_target_pairs={{0,3},{1,2},{2,1},{3,0},{4,7},{5,6},{6,5},{7,4},{8,11},{9,10},{10,... | collective-permute-start | bytes 1572872 | tf_op jit(solution)/shard_map/ppermute | solution.py:194
  137.4 56.7 %collective-permute-start.27 = (bf16[2,160,1024]{2,1,0:T(8,128)(2,1)}, bf16[2,160,1024]{2,1,0:T(8,128)(2,1)S(1)}, u32[]{:S(2)}, u32[]{:S(2)}) collective-permute-start(bf16[2,160,1024]{2,1,0:T(8,128)(2,1)} %get-tuple-element.94), channel_id=1, source_target_pairs={{0,1},{1,0},{2,3},{3,2},{4,5},{5,4},{6,7},{7,6},{8,9},{9,8},{10,11... | collective-permute-start | bytes 1966088 | tf_op jit(solution)/shard_map/ppermute | solution.py:194
  137.8 56.4 %collective-permute-start.28 = (bf16[2,160,1024]{2,1,0:T(8,128)(2,1)}, bf16[2,160,1024]{2,1,0:T(8,128)(2,1)S(1)}, u32[]{:S(2)}, u32[]{:S(2)}) collective-permute-start(bf16[2,160,1024]{2,1,0:T(8,128)(2,1)} %get-tuple-element.95), channel_id=1, source_target_pairs={{0,2},{1,3},{2,0},{3,1},{4,6},{5,7},{6,4},{7,5},{8,10},{9,11},{10,... | collective-permute-start | bytes 1966088 | tf_op jit(solution)/shard_map/ppermute | solution.py:194
  138.7 56.0 %collective-permute-start.29 = (bf16[2,160,1024]{2,1,0:T(8,128)(2,1)S(1)}, bf16[2,160,1024]{2,1,0:T(8,128)(2,1)S(1)}, u32[]{:S(2)}, u32[]{:S(2)}) collective-permute-start(bf16[2,160,1024]{2,1,0:T(8,128)(2,1)S(1)} %copy-done.46), channel_id=1, source_target_pairs={{0,3},{1,2},{2,1},{3,0},{4,7},{5,6},{6,5},{7,4},{8,11},{9,10},{10,... | collective-permute-start | bytes 1966088 | tf_op jit(solution)/shard_map/ppermute | solution.py:194
  139.4 56.0 %collective-permute-start.25 = (bf16[2,160,1024]{2,1,0:T(8,128)(2,1)}, bf16[2,160,1024]{2,1,0:T(8,128)(2,1)S(1)}, u32[]{:S(2)}, u32[]{:S(2)}) collective-permute-start(bf16[2,160,1024]{2,1,0:T(8,128)(2,1)} %get-tuple-element.92), channel_id=1, source_target_pairs={{0,2},{1,3},{2,0},{3,1},{4,6},{5,7},{6,4},{7,5},{8,10},{9,11},{10,... | collective-permute-start | bytes 1966088 | tf_op jit(solution)/shard_map/ppermute | solution.py:194
  148.3 59.4 %collective-permute-start.26 = (bf16[2,160,1024]{2,1,0:T(8,128)(2,1)}, bf16[2,160,1024]{2,1,0:T(8,128)(2,1)}, u32[]{:S(2)}, u32[]{:S(2)}) collective-permute-start(bf16[2,160,1024]{2,1,0:T(8,128)(2,1)} %get-tuple-element.93), channel_id=1, source_target_pairs={{0,3},{1,2},{2,1},{3,0},{4,7},{5,6},{6,5},{7,4},{8,11},{9,10},{10,... | collective-permute-start | bytes 1966088 | tf_op jit(solution)/shard_map/ppermute | solution.py:194
  195.4 37.2 %collective-permute-start.23 = (bf16[2,160,1024]{2,1,0:T(8,128)(2,1)}, bf16[2,160,1024]{2,1,0:T(8,128)(2,1)}, u32[]{:S(2)}, u32[]{:S(2)}) collective-permute-start(bf16[2,160,1024]{2,1,0:T(8,128)(2,1)} %get-tuple-element.91), channel_id=1, source_target_pairs={{0,3},{1,2},{2,1},{3,0},{4,7},{5,6},{6,5},{7,4},{8,11},{9,10},{10,... | collective-permute-start | bytes 1966088 | tf_op jit(solution)/shard_map/ppermute | solution.py:194
  220.5 40.1 %collective-permute-start.50 = (bf16[2,160,1024]{2,1,0:T(8,128)(2,1)}, bf16[2,160,1024]{2,1,0:T(8,128)(2,1)}, u32[]{:S(2)}, u32[]{:S(2)}) collective-permute-start(bf16[2,160,1024]{2,1,0:T(8,128)(2,1)} %get-tuple-element.121), channel_id=1, source_target_pairs={{0,3},{1,2},{2,1},{3,0},{4,7},{5,6},{6,5},{7,4},{8,11},{9,10},{10,... | collective-permute-start | bytes 1966088 | tf_op jit(solution)/shard_map/ppermute | solution.py:194
  221.3 39.4 %collective-permute-start.45 = (bf16[2,160,1024]{2,1,0:T(8,128)(2,1)}, bf16[2,160,1024]{2,1,0:T(8,128)(2,1)}, u32[]{:S(2)}, u32[]{:S(2)}) collective-permute-start(bf16[2,160,1024]{2,1,0:T(8,128)(2,1)} %get-tuple-element.116), channel_id=1, source_target_pairs={{0,1},{1,0},{2,3},{3,2},{4,5},{5,4},{6,7},{7,6},{8,9},{9,8},{10,11... | collective-permute-start | bytes 1966088 | tf_op jit(solution)/shard_map/ppermute | solution.py:194
  232.6 41.2 %collective-permute-start.46 = (bf16[2,160,1024]{2,1,0:T(8,128)(2,1)}, bf16[2,160,1024]{2,1,0:T(8,128)(2,1)}, u32[]{:S(2)}, u32[]{:S(2)}) collective-permute-start(bf16[2,160,1024]{2,1,0:T(8,128)(2,1)} %get-tuple-element.117), channel_id=1, source_target_pairs={{0,2},{1,3},{2,0},{3,1},{4,6},{5,7},{6,4},{7,5},{8,10},{9,11},{10,... | collective-permute-start | bytes 1966088 | tf_op jit(solution)/shard_map/ppermute | solution.py:194
  233.5 55.3 %collective-permute-start.47 = (bf16[2,160,1024]{2,1,0:T(8,128)(2,1)}, bf16[2,160,1024]{2,1,0:T(8,128)(2,1)}, u32[]{:S(2)}, u32[]{:S(2)}) collective-permute-start(bf16[2,160,1024]{2,1,0:T(8,128)(2,1)} %get-tuple-element.118), channel_id=1, source_target_pairs={{0,3},{1,2},{2,1},{3,0},{4,7},{5,6},{6,5},{7,4},{8,11},{9,10},{10,... | collective-permute-start | bytes 1966088 | tf_op jit(solution)/shard_map/ppermute | solution.py:194
  251.9 37.7 %collective-permute-start.39 = (bf16[2,96,1024]{2,1,0:T(8,128)(2,1)}, bf16[2,96,1024]{2,1,0:T(8,128)(2,1)S(1)}, u32[]{:S(2)}, u32[]{:S(2)}) collective-permute-start(bf16[2,96,1024]{2,1,0:T(8,128)(2,1)} %get-tuple-element.110), channel_id=1, source_target_pairs={{0,1},{1,0},{2,3},{3,2},{4,5},{5,4},{6,7},{7,6},{8,9},{9,8},{10,11... | collective-permute-start | bytes 1179656 | tf_op jit(solution)/shard_map/ppermute | solution.py:194
  260.7 35.2 %collective-permute-start.42 = (bf16[2,128,1024]{2,1,0:T(8,128)(2,1)}, bf16[2,128,1024]{2,1,0:T(8,128)(2,1)S(1)}, u32[]{:S(2)}, u32[]{:S(2)}) collective-permute-start(bf16[2,128,1024]{2,1,0:T(8,128)(2,1)} %get-tuple-element.113), channel_id=1, source_target_pairs={{0,1},{1,0},{2,3},{3,2},{4,5},{5,4},{6,7},{7,6},{8,9},{9,8},{10,11... | collective-permute-start | bytes 1572872 | tf_op jit(solution)/shard_map/ppermute | solution.py:194
  260.7 38.3 %collective-permute-start.43 = (bf16[2,128,1024]{2,1,0:T(8,128)(2,1)}, bf16[2,128,1024]{2,1,0:T(8,128)(2,1)S(1)}, u32[]{:S(2)}, u32[]{:S(2)}) collective-permute-start(bf16[2,128,1024]{2,1,0:T(8,128)(2,1)} %get-tuple-element.114), channel_id=1, source_target_pairs={{0,2},{1,3},{2,0},{3,1},{4,6},{5,7},{6,4},{7,5},{8,10},{9,11},{10,... | collective-permute-start | bytes 1572872 | tf_op jit(solution)/shard_map/ppermute | solution.py:194
  273.8 37.3 %collective-permute-start.44 = (bf16[2,128,1024]{2,1,0:T(8,128)(2,1)S(1)}, bf16[2,128,1024]{2,1,0:T(8,128)(2,1)S(1)}, u32[]{:S(2)}, u32[]{:S(2)}) collective-permute-start(bf16[2,128,1024]{2,1,0:T(8,128)(2,1)S(1)} %copy-done.47), channel_id=1, source_target_pairs={{0,3},{1,2},{2,1},{3,0},{4,7},{5,6},{6,5},{7,4},{8,11},{9,10},{10,... | collective-permute-start | bytes 1572872 | tf_op jit(solution)/shard_map/ppermute | solution.py:194
  289.6 38.3 %collective-permute-start.41 = (bf16[2,96,1024]{2,1,0:T(8,128)(2,1)}, bf16[2,96,1024]{2,1,0:T(8,128)(2,1)S(1)}, u32[]{:S(2)}, u32[]{:S(2)}) collective-permute-start(bf16[2,96,1024]{2,1,0:T(8,128)(2,1)} %get-tuple-element.112), channel_id=1, source_target_pairs={{0,3},{1,2},{2,1},{3,0},{4,7},{5,6},{6,5},{7,4},{8,11},{9,10},{10,... | collective-permute-start | bytes 1179656 | tf_op jit(solution)/shard_map/ppermute | solution.py:194
  295.9 35.6 %collective-permute-start.36 = (bf16[2,64,1024]{2,1,0:T(8,128)(2,1)}, bf16[2,64,1024]{2,1,0:T(8,128)(2,1)S(1)}, u32[]{:S(2)}, u32[]{:S(2)}) collective-permute-start(bf16[2,64,1024]{2,1,0:T(8,128)(2,1)} %get-tuple-element.107), channel_id=1, source_target_pairs={{0,1},{1,0},{2,3},{3,2},{4,5},{5,4},{6,7},{7,6},{8,9},{9,8},{10,11... | collective-permute-start | bytes 786440 | tf_op jit(solution)/shard_map/ppermute | solution.py:194
  (81 other events, 1223.8 us)

commit v2 on v1

v2 whole, which is shorter than its diff:
```python
import jax
import jax.numpy as jnp
from jax import lax
from jax.experimental import pallas as pl
from jax.experimental.pallas import tpu as pltpu
from jax.sharding import PartitionSpec as P


LANES, TILE, BLOCK = 128, 16, 80
SMALL = 8 << 20
GROUPS = ((4, 3), (3, 9, 8), (10, 10, 10, 10, 10, 9, 7, 4, 3))
TURNS = (1, 2)
AHEAD = 4
ROUTER_SENT, ROUTER_USED = 5, 9
DIRECT = 2
NEAR_DONE = 4


def plan(rows):
    total, at, done, groups = sum(map(sum, GROUPS)), 0, 0, []
    for lengths in GROUPS:
        chunks = []
        for length in lengths:
            done += length
            end = rows if done == total else rows * done // total // TILE * TILE
            if end > at:
                chunks.append((at, end - at))
            at = end
        if chunks:
            groups.append(chunks)
    return groups


def block_of(count):
    return max((u for u in range(TILE, BLOCK + 1, TILE) if count % u == 0), default=count)


def tree_sum(terms):
    terms = list(terms)
    while len(terms) > 1:
        terms = [sum(terms[i + 1 : i + 2], terms[i]) for i in range(0, len(terms), 2)]
    return terms[0]


def narrow(out, blocks, sums, base, places, own, peers, first, count, after):
    experts, n, rows, width = blocks.shape
    model = n * width
    step = block_of(count)
    steps = ([0] if own else []) + list(peers)
    m = len(steps)

    def body(places_ref, *refs):
        ins, sums_refs = refs[:m], refs[m : m + len(sums)]
        outs, factors = refs[-m - 1 : -1], refs[-1]
        e, i = pl.program_id(0), pl.program_id(1)

        @pl.when(i == 0)
        def _():
            inverse = 1.0 / (tree_sum(r[:, first - base : first - base + count] for r in sums_refs) / model)
            row = lax.broadcasted_iota(jnp.int32, inverse.shape, 0)
            for s, k in enumerate(steps):
                chosen = jnp.where(row == e * n + places_ref[k], inverse, 0.0)
                chosen = jnp.sum(chosen, axis=0, keepdims=True)
                factors[s] = jnp.broadcast_to(chosen, (LANES, count)).T

        rows_now = pl.ds(pl.multiple_of(i * step, step), step)
        for s in range(m):
            factor = factors[s, rows_now, :]
            for j in range(0, width, LANES):
                outs[s][0, :, j : j + LANES] = (ins[s][0, 0, :, j : j + LANES] * factor).astype(jnp.bfloat16)

    def reader(k):
        shape = (pl.Element(1), pl.Element(1), pl.Element(step), pl.Element(width))
        return pl.BlockSpec(shape, lambda e, i, p: (e, p[k], pl.multiple_of(first + i * step, TILE), 0))

    whole = pl.BlockSpec(sums[0].shape, lambda e, i, p: (0, 0))
    in_specs = [reader(k) for k in steps] + [whole] * len(sums)
    args = [blocks] * m + list(sums)
    aliases = {}
    if own and out is not None:
        aliases = {len(args) + 1: 0}
        args.append(out)
        in_specs.append(pl.BlockSpec(memory_space=pltpu.HBM))
    args += after
    in_specs += [pl.BlockSpec(memory_space=pl.ANY)] * len(after)
    out_shape = [jax.ShapeDtypeStruct((experts, count, width), jnp.bfloat16)] * len(peers)
    out_specs = [pl.BlockSpec((1, step, width), lambda e, i, p: (e, i, 0))] * len(peers)
    if own:
        out_shape = [jax.ShapeDtypeStruct((experts, rows, n * width), jnp.bfloat16)] + out_shape
        shape = (pl.Element(1), pl.Element(step), pl.Element(width))
        out_specs = [pl.BlockSpec(shape, lambda e, i, p: (e, pl.multiple_of(first + i * step, TILE), pl.multiple_of(p[n] * width, LANES)))] + out_specs
    bytes_moved = 6 * m * experts * count * width
    got = pl.pallas_call(
        body,
        out_shape=out_shape,
        grid_spec=pltpu.PrefetchScalarGridSpec(
            num_scalar_prefetch=1,
            grid=(experts, count // step),
            in_specs=in_specs,
            out_specs=out_specs,
            scratch_shapes=[pltpu.VMEM((m, count, LANES), jnp.float32)],
        ),
        input_output_aliases=aliases,
        compiler_params=pltpu.CompilerParams(vmem_limit_bytes=None if own else SMALL),
        cost_estimate=pl.CostEstimate(flops=bytes_moved, bytes_accessed=bytes_moved, transcendentals=0),
    )(places, *args)
    return (got[0] if own else out), dict(zip(peers, got[-len(peers) :]))


def narrow_opening(parts, sums, places, peers):
    experts, count, width = parts[0].shape
    m, n = len(peers), sums[0].shape[0] // experts

    def body(places_ref, *refs):
        ins, sums_refs, outs = refs[:m], refs[m : m + len(sums)], refs[-m:]
        inverse = 1.0 / (tree_sum(r[:, :count] for r in sums_refs) / (n * width))
        row = lax.broadcasted_iota(jnp.int32, inverse.shape, 0)
        for s, k in enumerate(peers):
            for e in range(experts):
                chosen = jnp.sum(jnp.where(row == e * n + places_ref[k], inverse, 0.0), axis=0, keepdims=True)
                factor = jnp.broadcast_to(chosen, (LANES, count)).T
                for j in range(0, width, LANES):
                    outs[s][e, :, j : j + LANES] = (ins[s][e, :, j : j + LANES] * factor).astype(jnp.bfloat16)

    bytes_moved = 6 * m * experts * count * width
    got = pl.pallas_call(
        body,
        out_shape=[jax.ShapeDtypeStruct((experts, count, width), jnp.bfloat16)] * m,
        grid_spec=pltpu.PrefetchScalarGridSpec(
            num_scalar_prefetch=1,
            grid=(1,),
            in_specs=[pl.BlockSpec(parts[0].shape, lambda i, p: (0, 0, 0))] * m
            + [pl.BlockSpec(sums[0].shape, lambda i, p: (0, 0))] * len(sums),
            out_specs=[pl.BlockSpec(parts[0].shape, lambda i, p: (0, 0, 0))] * m,
        ),
        compiler_params=pltpu.CompilerParams(vmem_limit_bytes=SMALL),
        cost_estimate=pl.CostEstimate(flops=bytes_moved, bytes_accessed=bytes_moved, transcendentals=0),
        name="narrow_opening",
    )(places, *parts, *sums)
    return dict(zip(peers, got))


def place(out, pieces, sources, first, last):
    experts, count, width = pieces[0].shape
    m = len(pieces)

    def body(sources_ref, *refs):
        ins, o = refs[:m], refs[m + 1]
        held, in_sems, out_sems = (ins, None, refs[-1]) if last else refs[m + 2 :]
        every = [(k, e) for k in range(m) for e in range(experts)]
        loads, stores = [], []
        for k, e in every:
            column = pl.multiple_of(sources_ref[k + 1] * width, width)
            target = o.at[e, pl.ds(first, count), pl.ds(column, width)]
            if last:
                stores.append(pltpu.make_async_copy(ins[k].at[e], target, out_sems.at[k, e]))
            else:
                loads.append(pltpu.make_async_copy(ins[k].at[e], held.at[k, e], in_sems.at[k, e]))
                stores.append(pltpu.make_async_copy(held.at[k, e], target, out_sems.at[k, e]))
        for load in loads:
            load.start()
        for s, store in enumerate(stores):
            if loads:
                loads[s].wait()
            store.start()
        for store in stores:
            store.wait()

    anywhere = pl.BlockSpec(memory_space=pltpu.HBM)
    bytes_moved = 4 * m * experts * count * width
    return pl.pallas_call(
        body,
        out_shape=jax.ShapeDtypeStruct(out.shape, out.dtype),
        grid_spec=pltpu.PrefetchScalarGridSpec(
            num_scalar_prefetch=1,
            grid=(),
            in_specs=[pl.BlockSpec(memory_space=pl.ANY) if last else anywhere] * m + [anywhere],
            out_specs=anywhere,
            scratch_shapes=[
                pltpu.VMEM((m, experts, count, width), jnp.bfloat16),
                pltpu.SemaphoreType.DMA((m, experts)),
                pltpu.SemaphoreType.DMA((m, experts)),
            ][2 * last :],
        ),
        input_output_aliases={m + 1: 0},
        compiler_params=pltpu.CompilerParams(vmem_limit_bytes=SMALL if last else None),
        cost_estimate=pl.CostEstimate(flops=bytes_moved, bytes_accessed=bytes_moved, transcendentals=0),
    )(sources, *pieces, out)


def per_device(master_down, router_weight, router_gain):
    n = lax.axis_size("rows")
    me = lax.axis_index("rows")
    experts, total_rows, width = master_down.shape
    rows = total_rows // n
    model = width * n
    groups = plan(rows)
    blocks = master_down.reshape(experts, n, rows, width)
    if n & (n - 1):
        hops = [[(i, (i + k) % n) for i in range(n)] for k in range(n)]
        targets = [(me + k) % n for k in range(n)]
        sources = [(me + n - k) % n for k in range(n)]
    else:
        hops = [[(i, i ^ k) for i in range(n)] for k in range(n)]
        targets = sources = [me ^ k for k in range(n)]
    target_list = jnp.stack(targets + [me]).astype(jnp.int32)
    source_list = target_list if sources is targets else jnp.stack(sources + [me]).astype(jnp.int32)
    paired = n % 2 == 0 and not n & (n - 1)
    near = [1] if paired else []
    far = [k for k in range(n - 1, 0, -1) if k not in near]

    def exchange(x, ks):
        return {k: lax.ppermute(x, "rows", hops[k]) for k in ks}

    def shared_sums(g, source):
        lo, hi = groups[g][0][0], sum(groups[g][-1])
        flat = source.reshape(experts * n, rows, width)
        sums = jnp.sum(jnp.abs(flat[:, lo:hi]), axis=2)
        if paired and g and g == len(groups) - 1:
            pair = sums + exchange(sums, near)[1]
            got = exchange(pair, [k for k in far if k % 2 == 0])
            return [pair] + [got[k] for k in sorted(got)]
        got = exchange(sums, far + near)
        return [sums] + [got[k] for k in range(1, n)]

    def send(pieces, ks):
        return {k: lax.ppermute(pieces[k], "rows", hops[k]) for k in ks}

    out, flying, after, router_rows = None, [], [], None
    serve_router = scale_down = None
    shared = [shared_sums(0, blocks)]
    c, chunks = 0, sum(map(len, groups))
    for g, group in enumerate(groups):
        base = group[0][0]
        turn = min(TURNS[g], len(group) - 1) if g + 1 < len(groups) else None
        for i, (first, count) in enumerate(group):
            if c == min(ROUTER_USED, chunks - 1):
                router_rows = lax.optimization_barrier((router_rows, token))[0]
                ordered = jnp.zeros((n,) + router_rows[0].shape, router_rows[0].dtype)
                for k in range(n):
                    ordered = lax.dynamic_update_index_in_dim(ordered, router_rows[k], sources[k], 0)
                row_router = ordered.reshape(n * router_weight.shape[0], router_weight.shape[1])
                serve_router = lax.all_gather(row_router, "owner", axis=1, tiled=True)
                totals = [tree_sum(s).reshape(experts, n, -1) for s in shared]
                totals = [lax.dynamic_index_in_dim(t, me, 1, keepdims=False) for t in totals]
                scale_down = jnp.concatenate(totals, axis=1) / model
                after = [serve_router, scale_down]
            opening = c == 0 and bool(far) and chunks > NEAR_DONE
            if opening:
                source = lax.optimization_barrier((blocks, shared[0][0]))[0]
                starts = [(0, targets[k], first, 0) for k in far]
                parts = [lax.dynamic_slice(source, s, (experts, 1, count, width))[:, 0] for s in starts]
                pieces = narrow_opening(lax.optimization_barrier(parts), shared[0], target_list, far)
            else:
                out, pieces = narrow(out, blocks, shared[g], base, target_list, True, far + near, first, count, after)
            after, token = [], pieces[(far + near)[0]]
            if i == turn:
                shared.append(shared_sums(g + 1, lax.optimization_barrier((blocks, token))[0]))
            if c == min(ROUTER_SENT, chunks - 2):
                weight, gain, _ = lax.optimization_barrier((router_weight, router_gain, token))
                part = (weight * gain[:, None]).astype(jnp.bfloat16)
                got = exchange(part, far + near)
                router_rows = [part] + [got[k] for k in range(1, n)]
            flying.append((send(pieces, far if opening else far + near), first))
            if c == NEAR_DONE and len(flying[0][0]) < n - 1:
                out, pieces = narrow(
                    out, blocks, shared[0], 0, target_list, True, near, groups[0][0][0], groups[0][0][1], []
                )
                flying[0][0].update(send(pieces, near))
            if len(flying) > AHEAD:
                got, at = flying.pop(0)
                out = place(out, [got[k] for k in range(1, n)], source_list, at, False)
            c += 1
    while flying:
        got, at = flying.pop(0)
        out = place(out, [got[k] for k in range(1, n)], source_list, at, len(flying) < DIRECT)
    return out, scale_down, serve_router


def solution(mesh):
    return jax.shard_map(
        per_device,
        mesh=mesh,
        in_specs=(P("owner", None, "rows"), P("rows", "owner"), P("rows")),
        out_specs=(P("owner", "rows", None), P("owner", "rows"), P()),
        check_vma=False,
    )
```

time: 345 us -> 382 us (1.11)
  waiting for transfers between devices: 123 us -> 169 us
  Pallas kernels: 117 us -> 110 us
    ppermute x51 -> x53, waiting for transfers between devices: 123 us -> 169 us  [the longest x42 142 us: send(): return {k: lax.ppermute(pieces[k], 'rows', hops[k]) for k in ks}]
    pallas_call x13 -> x15, Pallas kernels: 80.2 us -> 72.6 us  [the longest x14 71.9 us: narrow(): pl.pallas_call(body, out_shape=out_shape, grid_spec=pltpu.PrefetchScalarG...]
    ppermute x51 -> x53, starting transfers between devices: 36.1 us -> 39.6 us  [the longest x42 30.4 us: send(): return {k: lax.ppermute(pieces[k], 'rows', hops[k]) for k in ks}]
    pallas_call x13 -> x14, Pallas kernels: 37.1 us -> 37.2 us  [place(): pl.pallas_call(body, out_shape=jax.ShapeDtypeStruct(out.shape, out.dtype)...]
  transfers between devices with their start and end apart: 51 -> 53, of which waited for: 19 -> 21; matrix products, arithmetic and copies ran while one was open for 6% -> 1% of each run, Pallas kernels for 32% -> 24%
where the time goes in v2:
time: 382 us; the launch traced here: 380 us
  waiting for transfers between devices  169 us (44%)
  Pallas kernels  110 us (29%)
  starting transfers between devices  39.6 us (10%)
  blocking collectives  31 us (8%)
  other arithmetic  21.3 us (6%)
  local copies, waits for them, and re-layouts  6.94 us (2%)
    ppermute x42, waiting for transfers between devices, send(): return {k: lax.ppermute(pieces[k], 'rows', hops[k]) for k in ks}  142 us
    pallas_call x14, Pallas kernels, narrow(): pl.pallas_call(body, out_shape=out_shape, grid_spec=pltpu.PrefetchScalarG...  71.9 us
    pallas_call x14, Pallas kernels, place(): pl.pallas_call(body, out_shape=jax.ShapeDtypeStruct(out.shape, out.dtype)...  37.2 us
    all_gather x1, blocking collectives, per_device(): serve_router = lax.all_gather(row_router, 'owner', axis=1, tiled=True)  31 us
    ppermute x42, starting transfers between devices, send(): return {k: lax.ppermute(pieces[k], 'rows', hops[k]) for k in ks}  30.4 us
    ppermute x11, waiting for transfers between devices, exchange(): return {k: lax.ppermute(x, 'rows', hops[k]) for k in ks}  27.7 us
    reduce_sum x3, other arithmetic, shared_sums(): sums = jnp.sum(jnp.abs(flat[:, lo:hi]), axis=2)  20.6 us
    ppermute x11, starting transfers between devices, exchange(): return {k: lax.ppermute(x, 'rows', hops[k]) for k in ks}  9.19 us
  transfers between devices with their start and end apart: 53, of which 21 were waited for; matrix products, arithmetic and copies ran while one was open for 1% of the time, Pallas kernels for 24%

profile of v2, /device:TPU:0, one launch (start us, length us, event | category | flops | bytes accessed | tf_op | source)
XLA Modules:
  0.0 379.9 jit_solution(9820593638835601829)
XLA Ops:
  12.9 4.8 %fusion.1.refs_4_ = f32[8,320]{1,0:T(8,128)S(1)} fusion(f32[8,1600,1024]{2,1,0:T(8,128)} %bitcast.41), kind=kLoop, calls=%fused_computation.3 | loop fusion | flops 5240320 | bytes 10496000 | tf_op jit(solution)/shard_map/reduce_sum | solution.py:218
  25.3 6.7 %shard_map.60 = (bf16[2,1600,4096]{2,1,0:T(8,128)(2,1)}, bf16[2,144,1024]{2,1,0:T(8,128)(2,1)}, bf16[2,144,1024]{2,1,0:T(8,128)(2,1)}, bf16[2,144,1024]{2,1,0:T(8,128)(2,1)}) custom-call(s32[5]{0:T(128)} %stack.20.places_ref.sources_ref, f32[2,4,1600,1024]{3,2,1,0:T(8,128)} %bitcast.48, ...), custom_call_target="tpu_custom_call", output_to_operand_aliasing={{0}: (9, {})} | custom-call | flops 7077888 | bytes 7077888 | tf_op jit(solution)/shard_map/pallas_call | solution.py:93
  31.9 5.1 %shard_map.61 = (bf16[2,1600,4096]{2,1,0:T(8,128)(2,1)}, bf16[2,128,1024]{2,1,0:T(8,128)(2,1)}, bf16[2,128,1024]{2,1,0:T(8,128)(2,1)}, bf16[2,128,1024]{2,1,0:T(8,128)(2,1)}) custom-call(s32[5]{0:T(128)} %stack.20.places_ref.sources_ref, f32[2,4,1600,1024]{3,2,1,0:T(8,128)} %bitcast.50, ...), custom_call_target="tpu_custom_call", output_to_operand_aliasing={{0}: (9, {})} | custom-call | flops 6291456 | bytes 6291456 | tf_op jit(solution)/shard_map/pallas_call | solution.py:93
  37.1 13.4 %fusion = f32[8,1168]{1,0:T(8,128)S(1)} fusion(f32[8,1600,1024]{2,1,0:T(8,128)} %bitcast.54), kind=kLoop, calls=%fused_computation.1 | loop fusion | flops 19127168 | bytes 38310400 | tf_op jit(solution)/shard_map/reduce_sum | solution.py:218
  59.6 8.8 %collective-permute-done.7.refs_5_ = f32[8,1168]{1,0:T(8,128)S(1)} collective-permute-done((f32[8,1168]{1,0:T(8,128)S(1)}, f32[8,1168]{1,0:T(8,128)S(1)}, u32[]{:S(2)}, u32[]{:S(2)}) %collective-permute-start.7) | collective-permute-done | bytes 37408 | tf_op jit(solution)/shard_map/ppermute | solution.py:213
  77.7 5.6 %shard_map.64 = (bf16[2,1600,4096]{2,1,0:T(8,128)(2,1)}, bf16[2,160,1024]{2,1,0:T(8,128)(2,1)}, bf16[2,160,1024]{2,1,0:T(8,128)(2,1)}, bf16[2,160,1024]{2,1,0:T(8,128)(2,1)}) custom-call(s32[5]{0:T(128)} %stack.20.places_ref.sources_ref, f32[2,4,1600,1024]{3,2,1,0:T(8,128)} %bitcast.58, ...), custom_call_target="tpu_custom_call", output_to_operand_aliasing={{0}: (7, {})} | custom-call | flops 7864320 | bytes 7864320 | tf_op jit(solution)/shard_map/pallas_call | solution.py:93
  86.0 9.5 %collective-permute-done.13.refs_2_ = bf16[2,48,1024]{2,1,0:T(8,128)(2,1)S(1)} collective-permute-done((bf16[2,48,1024]{2,1,0:T(8,128)(2,1)S(1)}, bf16[2,48,1024]{2,1,0:T(8,128)(2,1)S(1)}, u32[]{:S(2)}, u32[]{:S(2)}) %collective-permute-start.13) | collective-permute-done | bytes 196640 | tf_op jit(solution)/shard_map/ppermute | solution.py:227
  97.1 11.1 %collective-permute-done.37 = bf16[1024,2]{0,1:T(2,128)(2,1)S(1)} collective-permute-done((bf16[1024,2]{0,1:T(2,128)(2,1)S(1)}, bf16[1024,2]{0,1:T(2,128)(2,1)S(1)}, u32[]{:S(2)}, u32[]{:S(2)}) %collective-permute-start.37) | collective-permute-done | bytes 4128 | tf_op jit(solution)/shard_map/ppermute | solution.py:213
  117.7 5.7 %shard_map.66 = (bf16[2,1600,4096]{2,1,0:T(8,128)(2,1)}, bf16[2,160,1024]{2,1,0:T(8,128)(2,1)}, bf16[2,160,1024]{2,1,0:T(8,128)(2,1)}, bf16[2,160,1024]{2,1,0:T(8,128)(2,1)}) custom-call(s32[5]{0:T(128)} %stack.20.places_ref.sources_ref, f32[2,4,1600,1024]{3,2,1,0:T(8,128)} %bitcast.63, ...), custom_call_target="tpu_custom_call", output_to_operand_aliasing={{0}: (7, {})} | custom-call | flops 7864320 | bytes 7864320 | tf_op jit(solution)/shard_map/pallas_call | solution.py:93
  123.5 3.7 collective-permute-done.34.refs_2_
  130.5 9.3 %collective-permute-done.10.refs_2_ = bf16[2,144,1024]{2,1,0:T(8,128)(2,1)} collective-permute-done((bf16[2,144,1024]{2,1,0:T(8,128)(2,1)}, bf16[2,144,1024]{2,1,0:T(8,128)(2,1)}, u32[]{:S(2)}, u32[]{:S(2)}) %collective-permute-start.10) | collective-permute-done | bytes 589856 | tf_op jit(solution)/shard_map/ppermute | solution.py:227
  144.6 5.6 %shard_map.68 = (bf16[2,1600,4096]{2,1,0:T(8,128)(2,1)}, bf16[2,160,1024]{2,1,0:T(8,128)(2,1)}, bf16[2,160,1024]{2,1,0:T(8,128)(2,1)}, bf16[2,160,1024]{2,1,0:T(8,128)(2,1)}) custom-call(s32[5]{0:T(128)} %stack.20.places_ref.sources_ref, f32[2,4,1600,1024]{3,2,1,0:T(8,128)} %bitcast.66, ...), custom_call_target="tpu_custom_call", output_to_operand_aliasing={{0}: (7, {})} | custom-call | flops 7864320 | bytes 7864320 | tf_op jit(solution)/shard_map/pallas_call | solution.py:93
  150.2 18.3 %collective-permute-done.30.refs_1_ = bf16[2,160,1024]{2,1,0:T(8,128)(2,1)S(1)} collective-permute-done((bf16[2,160,1024]{2,1,0:T(8,128)(2,1)}, bf16[2,160,1024]{2,1,0:T(8,128)(2,1)S(1)}, u32[]{:S(2)}, u32[]{:S(2)}) %collective-permute-start.30) | collective-permute-done | bytes 655392 | tf_op jit(solution)/shard_map/ppermute | solution.py:227
  173.6 5.7 %shard_map.70 = (bf16[2,1600,4096]{2,1,0:T(8,128)(2,1)}, bf16[2,160,1024]{2,1,0:T(8,128)(2,1)}, bf16[2,160,1024]{2,1,0:T(8,128)(2,1)}, bf16[2,160,1024]{2,1,0:T(8,128)(2,1)}) custom-call(s32[5]{0:T(128)} %stack.20.places_ref.sources_ref, f32[2,4,1600,1024]{3,2,1,0:T(8,128)} %bitcast.70, ...), custom_call_target="tpu_custom_call", output_to_operand_aliasing={{0}: (7, {})} | custom-call | flops 7864320 | bytes 7864320 | tf_op jit(solution)/shard_map/pallas_call | solution.py:93
  182.7 13.3 %collective-permute-done.28.refs_2_ = bf16[2,160,1024]{2,1,0:T(8,128)(2,1)} collective-permute-done((bf16[2,160,1024]{2,1,0:T(8,128)(2,1)}, bf16[2,160,1024]{2,1,0:T(8,128)(2,1)}, u32[]{:S(2)}, u32[]{:S(2)}) %collective-permute-start.28) | collective-permute-done | bytes 655392 | tf_op jit(solution)/shard_map/ppermute | solution.py:227
  198.3 31.0 %all-gather = bf16[8,2,4096]{2,1,0:T(2,128)(2,1)S(1)} all-gather(bf16[1,2,4096]{2,1,0:T(2,128)(2,1)S(1)} %bitcast.96), channel_id=1, replica_groups=mesh['owner'=8,'rows'=4] {'owner'}, dimensions={0}, use_global_device_ids=true | all-gather | bytes 147456 | tf_op jit(solution)/shard_map/all_gather | solution.py:243
  233.6 5.5 %shard_map.72 = (bf16[2,1600,4096]{2,1,0:T(8,128)(2,1)}, bf16[2,160,1024]{2,1,0:T(8,128)(2,1)}, bf16[2,160,1024]{2,1,0:T(8,128)(2,1)}, bf16[2,160,1024]{2,1,0:T(8,128)(2,1)}) custom-call(s32[5]{0:T(128)} %stack.20.places_ref.sources_ref, f32[2,4,1600,1024]{3,2,1,0:T(8,128)} %bitcast.74, ...), custom_call_target="tpu_custom_call", output_to_operand_aliasing={{0}: (7, {})} | custom-call | flops 7864320 | bytes 7864320 | tf_op jit(solution)/shard_map/pallas_call | solution.py:93
  242.1 6.6 %shard_map.74 = (bf16[2,1600,4096]{2,1,0:T(8,128)(2,1)}, bf16[2,144,1024]{2,1,0:T(8,128)(2,1)}, bf16[2,144,1024]{2,1,0:T(8,128)(2,1)}, bf16[2,144,1024]{2,1,0:T(8,128)(2,1)}) custom-call(s32[5]{0:T(128)} %stack.20.places_ref.sources_ref, f32[2,4,1600,1024]{3,2,1,0:T(8,128)} %bitcast.78, ...), custom_call_target="tpu_custom_call", output_to_operand_aliasing={{0}: (7, {})} | custom-call | flops 7077888 | bytes 7077888 | tf_op jit(solution)/shard_map/pallas_call | solution.py:93
  251.7 9.7 %shard_map.76 = (bf16[2,1600,4096]{2,1,0:T(8,128)(2,1)}, bf16[2,112,1024]{2,1,0:T(8,128)(2,1)}, bf16[2,112,1024]{2,1,0:T(8,128)(2,1)}, bf16[2,112,1024]{2,1,0:T(8,128)(2,1)}) custom-call(s32[5]{0:T(128)} %stack.20.places_ref.sources_ref, f32[2,4,1600,1024]{3,2,1,0:T(8,128)} %bitcast.82, ...), custom_call_target="tpu_custom_call", output_to_operand_aliasing={{0}: (7, {})} | custom-call | flops 5505024 | bytes 5505024 | tf_op jit(solution)/shard_map/pallas_call | solution.py:93
  271.8 12.6 %collective-permute-done.22.refs_2_ = bf16[2,160,1024]{2,1,0:T(8,128)(2,1)S(1)} collective-permute-done((bf16[2,160,1024]{2,1,0:T(8,128)(2,1)S(1)}, bf16[2,160,1024]{2,1,0:T(8,128)(2,1)S(1)}, u32[]{:S(2)}, u32[]{:S(2)}) %collective-permute-start.22) | collective-permute-done | bytes 655392 | tf_op jit(solution)/shard_map/ppermute | solution.py:227
  286.3 13.4 %collective-permute-done.51.refs_1_ = bf16[2,160,1024]{2,1,0:T(8,128)(2,1)S(1)} collective-permute-done((bf16[2,160,1024]{2,1,0:T(8,128)(2,1)}, bf16[2,160,1024]{2,1,0:T(8,128)(2,1)S(1)}, u32[]{:S(2)}, u32[]{:S(2)}) %collective-permute-start.51) | collective-permute-done | bytes 655392 | tf_op jit(solution)/shard_map/ppermute | solution.py:227
  299.7 12.8 %collective-permute-done.52.refs_2_ = bf16[2,160,1024]{2,1,0:T(8,128)(2,1)S(1)} collective-permute-done((bf16[2,160,1024]{2,1,0:T(8,128)(2,1)}, bf16[2,160,1024]{2,1,0:T(8,128)(2,1)S(1)}, u32[]{:S(2)}, u32[]{:S(2)}) %collective-permute-start.52) | collective-permute-done | bytes 655392 | tf_op jit(solution)/shard_map/ppermute | solution.py:227
  314.9 33.9 %collective-permute-done.45.refs_1_ = bf16[2,112,1024]{2,1,0:T(8,128)(2,1)S(1)} collective-permute-done((bf16[2,112,1024]{2,1,0:T(8,128)(2,1)}, bf16[2,112,1024]{2,1,0:T(8,128)(2,1)S(1)}, u32[]{:S(2)}, u32[]{:S(2)}) %collective-permute-start.45) | collective-permute-done | bytes 458784 | tf_op jit(solution)/shard_map/ppermute | solution.py:227
  349.7 7.7 %collective-permute-done.46.refs_2_ = bf16[2,112,1024]{2,1,0:T(8,128)(2,1)S(1)} collective-permute-done((bf16[2,112,1024]{2,1,0:T(8,128)(2,1)}, bf16[2,112,1024]{2,1,0:T(8,128)(2,1)S(1)}, u32[]{:S(2)}, u32[]{:S(2)}) %collective-permute-start.46) | collective-permute-done | bytes 458784 | tf_op jit(solution)/shard_map/ppermute | solution.py:227
  (279 shorter events, 118.0 us)
Async XLA Ops:
  74.0 40.0 %collective-permute-start.32 = (bf16[2,128,1024]{2,1,0:T(8,128)(2,1)}, bf16[2,128,1024]{2,1,0:T(8,128)(2,1)S(1)}, u32[]{:S(2)}, u32[]{:S(2)}) collective-permute-start(bf16[2,128,1024]{2,1,0:T(8,128)(2,1)} %get-tuple-element.108), channel_id=1, source_target_pairs={{0,1},{1,0},{2,3},{3,2},{4,5},{5,4},{6,7},{7,6},{8,9},{9,8},{10,11... | collective-permute-start | bytes 1572872 | tf_op jit(solution)/shard_map/ppermute | solution.py:227
  74.3 40.1 %collective-permute-start.33 = (bf16[2,128,1024]{2,1,0:T(8,128)(2,1)}, bf16[2,128,1024]{2,1,0:T(8,128)(2,1)S(1)}, u32[]{:S(2)}, u32[]{:S(2)}) collective-permute-start(bf16[2,128,1024]{2,1,0:T(8,128)(2,1)} %get-tuple-element.109), channel_id=1, source_target_pairs={{0,2},{1,3},{2,0},{3,1},{4,6},{5,7},{6,4},{7,5},{8,10},{9,11},{10,... | collective-permute-start | bytes 1572872 | tf_op jit(solution)/shard_map/ppermute | solution.py:227
  84.4 44.5 %collective-permute-start.8 = (bf16[2,144,1024]{2,1,0:T(8,128)(2,1)}, bf16[2,144,1024]{2,1,0:T(8,128)(2,1)S(1)}, u32[]{:S(2)}, u32[]{:S(2)}) collective-permute-start(bf16[2,144,1024]{2,1,0:T(8,128)(2,1)} %get-tuple-element.77), channel_id=1, source_target_pairs={{0,1},{1,0},{2,3},{3,2},{4,5},{5,4},{6,7},{7,6},{8,9},{9,8},{10,11... | collective-permute-start | bytes 1769480 | tf_op jit(solution)/shard_map/ppermute | solution.py:227
  85.1 44.6 %collective-permute-start.9 = (bf16[2,144,1024]{2,1,0:T(8,128)(2,1)}, bf16[2,144,1024]{2,1,0:T(8,128)(2,1)S(1)}, u32[]{:S(2)}, u32[]{:S(2)}) collective-permute-start(bf16[2,144,1024]{2,1,0:T(8,128)(2,1)} %get-tuple-element.78), channel_id=1, source_target_pairs={{0,2},{1,3},{2,0},{3,1},{4,6},{5,7},{6,4},{7,5},{8,10},{9,11},{10,... | collective-permute-start | bytes 1769480 | tf_op jit(solution)/shard_map/ppermute | solution.py:227
  114.0 27.1 %collective-permute-start.29 = (bf16[2,160,1024]{2,1,0:T(8,128)(2,1)}, bf16[2,160,1024]{2,1,0:T(8,128)(2,1)S(1)}, u32[]{:S(2)}, u32[]{:S(2)}) collective-permute-start(bf16[2,160,1024]{2,1,0:T(8,128)(2,1)} %get-tuple-element.105), channel_id=1, source_target_pairs={{0,1},{1,0},{2,3},{3,2},{4,5},{5,4},{6,7},{7,6},{8,9},{9,8},{10,11... | collective-permute-start | bytes 1966088 | tf_op jit(solution)/shard_map/ppermute | solution.py:227
  127.2 41.3 %collective-permute-start.31 = (bf16[2,160,1024]{2,1,0:T(8,128)(2,1)}, bf16[2,160,1024]{2,1,0:T(8,128)(2,1)S(1)}, u32[]{:S(2)}, u32[]{:S(2)}) collective-permute-start(bf16[2,160,1024]{2,1,0:T(8,128)(2,1)} %get-tuple-element.107), channel_id=1, source_target_pairs={{0,3},{1,2},{2,1},{3,0},{4,7},{5,6},{6,5},{7,4},{8,11},{9,10},{10,... | collective-permute-start | bytes 1966088 | tf_op jit(solution)/shard_map/ppermute | solution.py:227
  128.8 39.7 %collective-permute-start.30 = (bf16[2,160,1024]{2,1,0:T(8,128)(2,1)}, bf16[2,160,1024]{2,1,0:T(8,128)(2,1)S(1)}, u32[]{:S(2)}, u32[]{:S(2)}) collective-permute-start(bf16[2,160,1024]{2,1,0:T(8,128)(2,1)} %get-tuple-element.106), channel_id=1, source_target_pairs={{0,2},{1,3},{2,0},{3,1},{4,6},{5,7},{6,4},{7,5},{8,10},{9,11},{10,... | collective-permute-start | bytes 1966088 | tf_op jit(solution)/shard_map/ppermute | solution.py:227
  130.5 39.3 %collective-permute-start.26 = (bf16[2,160,1024]{2,1,0:T(8,128)(2,1)}, bf16[2,160,1024]{2,1,0:T(8,128)(2,1)S(1)}, u32[]{:S(2)}, u32[]{:S(2)}) collective-permute-start(bf16[2,160,1024]{2,1,0:T(8,128)(2,1)} %get-tuple-element.102), channel_id=1, source_target_pairs={{0,1},{1,0},{2,3},{3,2},{4,5},{5,4},{6,7},{7,6},{8,9},{9,8},{10,11... | collective-permute-start | bytes 1966088 | tf_op jit(solution)/shard_map/ppermute | solution.py:227
  139.9 42.8 %collective-permute-start.27 = (bf16[2,160,1024]{2,1,0:T(8,128)(2,1)}, bf16[2,160,1024]{2,1,0:T(8,128)(2,1)}, u32[]{:S(2)}, u32[]{:S(2)}) collective-permute-start(bf16[2,160,1024]{2,1,0:T(8,128)(2,1)} %get-tuple-element.103), channel_id=1, source_target_pairs={{0,2},{1,3},{2,0},{3,1},{4,6},{5,7},{6,4},{7,5},{8,10},{9,11},{10,... | collective-permute-start | bytes 1966088 | tf_op jit(solution)/shard_map/ppermute | solution.py:227
  141.1 55.0 %collective-permute-start.28 = (bf16[2,160,1024]{2,1,0:T(8,128)(2,1)}, bf16[2,160,1024]{2,1,0:T(8,128)(2,1)}, u32[]{:S(2)}, u32[]{:S(2)}) collective-permute-start(bf16[2,160,1024]{2,1,0:T(8,128)(2,1)} %get-tuple-element.104), channel_id=1, source_target_pairs={{0,3},{1,2},{2,1},{3,0},{4,7},{5,6},{6,5},{7,4},{8,11},{9,10},{10,... | collective-permute-start | bytes 1966088 | tf_op jit(solution)/shard_map/ppermute | solution.py:227
  168.5 92.9 %collective-permute-start.23 = (bf16[2,160,1024]{2,1,0:T(8,128)(2,1)}, bf16[2,160,1024]{2,1,0:T(8,128)(2,1)}, u32[]{:S(2)}, u32[]{:S(2)}) collective-permute-start(bf16[2,160,1024]{2,1,0:T(8,128)(2,1)} %get-tuple-element.99), channel_id=1, source_target_pairs={{0,1},{1,0},{2,3},{3,2},{4,5},{5,4},{6,7},{7,6},{8,9},{9,8},{10,11... | collective-permute-start | bytes 1966088 | tf_op jit(solution)/shard_map/ppermute | solution.py:227
  168.6 92.9 %collective-permute-start.24 = (bf16[2,160,1024]{2,1,0:T(8,128)(2,1)}, bf16[2,160,1024]{2,1,0:T(8,128)(2,1)}, u32[]{:S(2)}, u32[]{:S(2)}) collective-permute-start(bf16[2,160,1024]{2,1,0:T(8,128)(2,1)} %get-tuple-element.100), channel_id=1, source_target_pairs={{0,2},{1,3},{2,0},{3,1},{4,6},{5,7},{6,4},{7,5},{8,10},{9,11},{10,... | collective-permute-start | bytes 1966088 | tf_op jit(solution)/shard_map/ppermute | solution.py:227
  169.8 91.6 %collective-permute-start.25 = (bf16[2,160,1024]{2,1,0:T(8,128)(2,1)}, bf16[2,160,1024]{2,1,0:T(8,128)(2,1)}, u32[]{:S(2)}, u32[]{:S(2)}) collective-permute-start(bf16[2,160,1024]{2,1,0:T(8,128)(2,1)} %get-tuple-element.101), channel_id=1, source_target_pairs={{0,3},{1,2},{2,1},{3,0},{4,7},{5,6},{6,5},{7,4},{8,11},{9,10},{10,... | collective-permute-start | bytes 1966088 | tf_op jit(solution)/shard_map/ppermute | solution.py:227
  182.7 87.9 %collective-permute-start.20 = (bf16[2,160,1024]{2,1,0:T(8,128)(2,1)}, bf16[2,160,1024]{2,1,0:T(8,128)(2,1)}, u32[]{:S(2)}, u32[]{:S(2)}) collective-permute-start(bf16[2,160,1024]{2,1,0:T(8,128)(2,1)} %get-tuple-element.96), channel_id=1, source_target_pairs={{0,1},{1,0},{2,3},{3,2},{4,5},{5,4},{6,7},{7,6},{8,9},{9,8},{10,11... | collective-permute-start | bytes 1966088 | tf_op jit(solution)/shard_map/ppermute | solution.py:227
  196.0 75.1 %collective-permute-start.21 = (bf16[2,160,1024]{2,1,0:T(8,128)(2,1)}, bf16[2,160,1024]{2,1,0:T(8,128)(2,1)}, u32[]{:S(2)}, u32[]{:S(2)}) collective-permute-start(bf16[2,160,1024]{2,1,0:T(8,128)(2,1)} %get-tuple-element.97), channel_id=1, source_target_pairs={{0,2},{1,3},{2,0},{3,1},{4,6},{5,7},{6,4},{7,5},{8,10},{9,11},{10,... | collective-permute-start | bytes 1966088 | tf_op jit(solution)/shard_map/ppermute | solution.py:227
  269.7 30.0 %collective-permute-start.51 = (bf16[2,160,1024]{2,1,0:T(8,128)(2,1)}, bf16[2,160,1024]{2,1,0:T(8,128)(2,1)S(1)}, u32[]{:S(2)}, u32[]{:S(2)}) collective-permute-start(bf16[2,160,1024]{2,1,0:T(8,128)(2,1)} %get-tuple-element.134), channel_id=1, source_target_pairs={{0,2},{1,3},{2,0},{3,1},{4,6},{5,7},{6,4},{7,5},{8,10},{9,11},{10,... | collective-permute-start | bytes 1966088 | tf_op jit(solution)/shard_map/ppermute | solution.py:227
  270.5 42.0 %collective-permute-start.52 = (bf16[2,160,1024]{2,1,0:T(8,128)(2,1)}, bf16[2,160,1024]{2,1,0:T(8,128)(2,1)S(1)}, u32[]{:S(2)}, u32[]{:S(2)}) collective-permute-start(bf16[2,160,1024]{2,1,0:T(8,128)(2,1)} %get-tuple-element.135), channel_id=1, source_target_pairs={{0,3},{1,2},{2,1},{3,0},{4,7},{5,6},{6,5},{7,4},{8,11},{9,10},{10,... | collective-permute-start | bytes 1966088 | tf_op jit(solution)/shard_map/ppermute | solution.py:227
  271.2 42.2 %collective-permute-start.44 = (bf16[2,112,1024]{2,1,0:T(8,128)(2,1)}, bf16[2,112,1024]{2,1,0:T(8,128)(2,1)S(1)}, u32[]{:S(2)}, u32[]{:S(2)}) collective-permute-start(bf16[2,112,1024]{2,1,0:T(8,128)(2,1)} %get-tuple-element.127), channel_id=1, source_target_pairs={{0,1},{1,0},{2,3},{3,2},{4,5},{5,4},{6,7},{7,6},{8,9},{9,8},{10,11... | collective-permute-start | bytes 1376264 | tf_op jit(solution)/shard_map/ppermute | solution.py:227
  284.4 81.5 %collective-permute-start.47 = (bf16[2,144,1024]{2,1,0:T(8,128)(2,1)}, bf16[2,144,1024]{2,1,0:T(8,128)(2,1)}, u32[]{:S(2)}, u32[]{:S(2)}) collective-permute-start(bf16[2,144,1024]{2,1,0:T(8,128)(2,1)} %get-tuple-element.130), channel_id=1, source_target_pairs={{0,1},{1,0},{2,3},{3,2},{4,5},{5,4},{6,7},{7,6},{8,9},{9,8},{10,11... | collective-permute-start | bytes 1769480 | tf_op jit(solution)/shard_map/ppermute | solution.py:227
  285.5 80.6 %collective-permute-start.48 = (bf16[2,144,1024]{2,1,0:T(8,128)(2,1)}, bf16[2,144,1024]{2,1,0:T(8,128)(2,1)}, u32[]{:S(2)}, u32[]{:S(2)}) collective-permute-start(bf16[2,144,1024]{2,1,0:T(8,128)(2,1)} %get-tuple-element.131), channel_id=1, source_target_pairs={{0,2},{1,3},{2,0},{3,1},{4,6},{5,7},{6,4},{7,5},{8,10},{9,11},{10,... | collective-permute-start | bytes 1769480 | tf_op jit(solution)/shard_map/ppermute | solution.py:227
  299.7 67.6 %collective-permute-start.49 = (bf16[2,144,1024]{2,1,0:T(8,128)(2,1)}, bf16[2,144,1024]{2,1,0:T(8,128)(2,1)}, u32[]{:S(2)}, u32[]{:S(2)}) collective-permute-start(bf16[2,144,1024]{2,1,0:T(8,128)(2,1)} %get-tuple-element.132), channel_id=1, source_target_pairs={{0,3},{1,2},{2,1},{3,0},{4,7},{5,6},{6,5},{7,4},{8,11},{9,10},{10,... | collective-permute-start | bytes 1769480 | tf_op jit(solution)/shard_map/ppermute | solution.py:227
  312.5 36.3 %collective-permute-start.45 = (bf16[2,112,1024]{2,1,0:T(8,128)(2,1)}, bf16[2,112,1024]{2,1,0:T(8,128)(2,1)S(1)}, u32[]{:S(2)}, u32[]{:S(2)}) collective-permute-start(bf16[2,112,1024]{2,1,0:T(8,128)(2,1)} %get-tuple-element.128), channel_id=1, source_target_pairs={{0,2},{1,3},{2,0},{3,1},{4,6},{5,7},{6,4},{7,5},{8,10},{9,11},{10,... | collective-permute-start | bytes 1376264 | tf_op jit(solution)/shard_map/ppermute | solution.py:227
  313.4 44.1 %collective-permute-start.46 = (bf16[2,112,1024]{2,1,0:T(8,128)(2,1)}, bf16[2,112,1024]{2,1,0:T(8,128)(2,1)S(1)}, u32[]{:S(2)}, u32[]{:S(2)}) collective-permute-start(bf16[2,112,1024]{2,1,0:T(8,128)(2,1)} %get-tuple-element.129), channel_id=1, source_target_pairs={{0,3},{1,2},{2,1},{3,0},{4,7},{5,6},{6,5},{7,4},{8,11},{9,10},{10,... | collective-permute-start | bytes 1376264 | tf_op jit(solution)/shard_map/ppermute | solution.py:227
  348.9 28.0 %collective-permute-start.42 = (bf16[2,64,1024]{2,1,0:T(8,128)(2,1)}, bf16[2,64,1024]{2,1,0:T(8,128)(2,1)S(1)}, u32[]{:S(2)}, u32[]{:S(2)}) collective-permute-start(bf16[2,64,1024]{2,1,0:T(8,128)(2,1)} %get-tuple-element.125), channel_id=1, source_target_pairs={{0,2},{1,3},{2,0},{3,1},{4,6},{5,7},{6,4},{7,5},{8,10},{9,11},{10,... | collective-permute-start | bytes 786440 | tf_op jit(solution)/shard_map/ppermute | solution.py:227
  (97 other events, 1298.5 us)
